TPU v7x, 32 devices: a whole 2x2x4 slice. The times are simulated.
32 devices in a mesh: task: 2 (over x), batch: 16 (over z, y, core).
Axes of the slice: x: 2, y: 2, z: 4, core: 2. Of those that a mesh axis runs over, the one named last changes fastest.
Arguments:
- pooled: bfloat16 [12288, 3328], P('batch'), may hold values from -6 to 6
- gate_weight: bfloat16 [3328, 8, 4], P(None, 'task'), may hold values from -0.21875 to 0.21875
- w_first: bfloat16 [8, 3328, 1024], P('task', 'batch'), may hold values from -0.15625 to 0.15625
- w_second: bfloat16 [8, 1024, 512], P('task', 'batch'), may hold values from -0.25 to 0.25
- w_third: bfloat16 [8, 512, 256], P('task', 'batch'), may hold values from -0.375 to 0.375
- tower_hidden: bfloat16 [4, 256, 128], P('task'), may hold values from -0.5 to 0.5
- tower_out: bfloat16 [4, 128], P('task'), may hold values from -0.75 to 0.75
Outputs:
- task_logits: float32 [12288, 4], P('batch', 'task')
All inputs are finite; a program needn't handle non-finite values.
Results may differ from a plain program's by a relative error of at most 0.02.
Values may be sent and summed in bfloat16 or wider, within the bound.
A program may use at most 128 MiB of HBM per device.

v0:
```python
import jax
import jax.numpy as jnp
from jax import lax
from jax.sharding import PartitionSpec as P


def per_device(pooled, gate_weight, w_first, w_second, w_third, tower_hidden, tower_out):
    tok_rows = pooled.shape[0]
    width_in = pooled.shape[1]
    local_experts = w_first.shape[0]
    all_tasks = gate_weight.shape[2]
    own_tasks = tower_hidden.shape[0]
    gathered = lax.all_gather(w_first, "batch", axis=1, tiled=True)
    summed = jnp.einsum("tr,erh->eth", pooled, gathered, preferred_element_type=jnp.float32)
    first = jax.nn.relu(summed).astype(jnp.bfloat16)
    logits = jnp.dot(
        pooled,
        gate_weight.reshape(width_in, local_experts * all_tasks),
        preferred_element_type=jnp.float32,
    )
    weights = jnp.exp(logits.reshape(tok_rows, local_experts, all_tasks))
    gate_total = jnp.sum(weights, axis=1)
    columns = first
    second = jax.nn.relu(
        jnp.einsum(
            "etr,erh->eth",
            columns,
            lax.all_gather(w_second, "batch", axis=1, tiled=True),
            preferred_element_type=jnp.float32,
        )
    ).astype(jnp.bfloat16)
    columns = second
    expert_out = jax.nn.relu(
        jnp.einsum(
            "etr,erh->eth",
            columns,
            lax.all_gather(w_third, "batch", axis=1, tiled=True),
            preferred_element_type=jnp.float32,
        )
    ).astype(jnp.bfloat16)
    numer = jnp.einsum("tek,eth->tkh", weights, expert_out.astype(jnp.float32))
    numer_all, total_all = (
        lax.psum(numer.astype(jnp.bfloat16), "task").astype(jnp.float32),
        lax.psum(gate_total.astype(jnp.bfloat16), "task").astype(jnp.float32),
    )
    first_task = lax.axis_index("task") * own_tasks
    numer_own = lax.dynamic_slice_in_dim(numer_all, first_task, own_tasks, 1)
    total_own = lax.dynamic_slice_in_dim(total_all, first_task, own_tasks, 1)
    mix = (numer_own / total_own[:, :, None]).astype(jnp.bfloat16)
    tower = jax.nn.relu(
        jnp.einsum("tkh,khm->tkm", mix, tower_hidden, preferred_element_type=jnp.float32)
    ).astype(jnp.bfloat16)
    return jnp.einsum("tkm,km->tk", tower, tower_out, preferred_element_type=jnp.float32)


def solution(mesh):
    placed = (
        P("batch", None),
        P(None, "task", None),
        P("task", "batch", None),
        P("task", "batch", None),
        P("task", "batch", None),
        P("task", None, None),
        P("task", None),
    )
    return jax.shard_map(
        per_device, mesh=mesh, in_specs=placed, out_specs=P("batch", "task"), check_vma=False
    )
```

profile of v0, /device:TPU:0, one launch (start us, length us, event | category | flops | bytes accessed | tf_op | source)
XLA Modules:
  0.0 307.8 jit_solution(7706464251963237315)
XLA Ops:
  6.5 0.0 copy-start
  6.5 0.0 all-gather.6.cloned.1.call-start
  6.5 0.7 all-gather.6.cloned.1.call-update
  7.3 0.0 all-gather.4.cloned.1.call-start
  7.3 0.7 all-gather.4.cloned.1.call-update
  8.0 0.0 all-gather.8.cloned.1.call-start
  8.1 0.7 all-gather.8.cloned.1.call-update
  8.7 0.0 all-reduce.2.cloned.1.call-start
  8.8 0.9 reshape.6
  9.8 4.1 %fusion.27 = (bf16[768,4]{0,1:T(4,128)(2,1)S(1)}, bf16[768,4,4]{0,2,1:T(4,128)(2,1)S(1)}) fusion(bf16[4,4,3328]{2,1,0:T(4,128)(2,1)S(1)} %dot_general.26, bf16[768,3328]{1,0:T(8,128)(2,1)} %param.7), kind=kOutput, calls=%fused_computation.28 | convolution fusion | flops 81810432 | bytes 5249024 | tf_op jit(solution)/shard_map/dot_general | solution.py:16
  13.8 0.6 copy.9
  14.4 48.2 %all-gather.6.cloned.1.call-done = bf16[4,1024,512]{2,1,0:T(8,128)(2,1)} async-done(((bf16[4,64,512]{2,1,0:T(8,128)(2,1)}), bf16[4,1024,512]{2,1,0:T(8,128)(2,1)}) %all-gather.6.cloned.1.call-update) | async-done | bytes 4194320 | tf_op jit(solution)/shard_map/all_gather | solution.py:28
  62.7 138.5 %all-gather.4.cloned.1.call-done = bf16[4,3328,1024]{2,1,0:T(8,128)(2,1)} async-done(((bf16[4,208,1024]{2,1,0:T(8,128)(2,1)}), bf16[4,3328,1024]{2,1,0:T(8,128)(2,1)}) %all-gather.4.cloned.1.call-update) | async-done | bytes 27262992 | tf_op jit(solution)/shard_map/all_gather | solution.py:13
  201.2 36.5 %fusion = bf16[4,768,512]{2,1,0:T(8,128)(2,1)} fusion(bf16[4,1024,512]{2,1,0:T(8,128)(2,1)} %all-gather.6.cloned.1.call-done, bf16[4,3328,1024]{2,1,0:T(8,128)(2,1)} %all-gather.4.cloned.1.call-done, bf16[768,3328]{1,0:T(8,128)(2,1)} %param.7), kind=kOutput, calls=%fused_computation.1 | convolution fusion | flops 24165482496 | bytes 39714816 | tf_op jit(solution)/shard_map/etr,erh->eth/dot_general | solution.py:25
  237.7 3.5 %all-gather.8.cloned.1.call-done = bf16[4,512,256]{2,1,0:T(8,128)(2,1)} async-done(((bf16[4,32,256]{2,1,0:T(8,128)(2,1)}), bf16[4,512,256]{2,1,0:T(8,128)(2,1)}) %all-gather.8.cloned.1.call-update) | async-done | bytes 1048592 | tf_op jit(solution)/shard_map/all_gather | solution.py:37
  241.3 3.2 %maximum_convert_fusion.4 = bf16[4,768,256]{2,1,0:T(8,128)(2,1)S(1)} fusion(bf16[4,512,256]{2,1,0:T(8,128)(2,1)} %all-gather.8.cloned.1.call-done, bf16[4,768,512]{2,1,0:T(8,128)(2,1)} %fusion), kind=kOutput, calls=%fused_computation.9 | convolution fusion | flops 811597824 | bytes 5767168 | tf_op jit(solution)/shard_map/etr,erh->eth/dot_general | solution.py:34
  244.4 0.0 copy-start.1
  244.4 2.6 convolution_convert_fusion
  247.0 0.0 all-reduce.2.cloned.1.call-update
  247.0 5.0 %psum.15 = bf16[768,4]{0,1:T(4,128)(2,1)S(1)} all-reduce(bf16[768,4]{0,1:T(4,128)(2,1)S(1)} %get-tuple-element.5), channel_id=1, replica_groups=mesh['task'=2,'batch'=16] {'task'}, use_global_device_ids=true, to_apply=%region_2.3 | all-reduce | flops 3072 | bytes 12288 | tf_op jit(solution)/shard_map/psum | solution.py:44
  252.1 0.2 copy.8
  252.2 45.5 %all-reduce.2.cloned.1.call-done = bf16[768,4,256]{2,1,0:T(4,128)(2,1)} async-done(((bf16[768,4,256]{2,1,0:T(4,128)(2,1)}), bf16[768,4,256]{2,1,0:T(4,128)(2,1)}) %all-reduce.2.cloned.1.call-update) | async-done | bytes 1572880 | tf_op jit(solution)/shard_map/psum | solution.py:43
  297.7 2.5 fusion.13
  300.2 0.0 copy-done
  300.2 0.0 copy-done.1
  300.2 0.5 fusion.16
  300.7 0.6 copy.22
  (2 shorter events, 0.0 us)
Async XLA Ops:
  6.5 293.6 %copy-start = (bf16[2,256,128]{2,1,0:T(8,128)(2,1)S(1)}, bf16[2,256,128]{2,1,0:T(8,128)(2,1)}, u32[]{:S(2)}) copy-start(bf16[2,256,128]{2,1,0:T(8,128)(2,1)} %param.12) | copy-start | bytes 393220
  6.5 56.1 %all-gather.6.cloned.1.call-start = ((), (), s32[]{:S(2)}) async-start(), calls=%async_computation.1 | async-start | bytes 4456448 | tf_op jit(solution)/shard_map/all_gather | solution.py:28
  7.3 193.9 %all-gather.4.cloned.1.call-start = ((), (), s32[]{:S(2)}) async-start(), calls=%async_computation | async-start | bytes 28966912 | tf_op jit(solution)/shard_map/all_gather | solution.py:13
  8.0 233.3 %all-gather.8.cloned.1.call-start = ((), (), s32[]{:S(2)}) async-start(), calls=%async_computation.2 | async-start | bytes 1114112 | tf_op jit(solution)/shard_map/all_gather | solution.py:37
  8.7 289.0 %all-reduce.2.cloned.1.call-start = ((), (), s32[]{:S(2)}) async-start(), calls=%async_computation.3 | async-start | bytes 3145728 | tf_op jit(solution)/shard_map/psum | solution.py:43
  244.4 55.8 %copy-start.1 = (bf16[2,128]{1,0:T(2,128)(2,1)S(1)}, bf16[2,128]{1,0:T(2,128)(2,1)}, u32[]{:S(2)}) copy-start(bf16[2,128]{1,0:T(2,128)(2,1)} %param.13) | copy-start | bytes 1540
Sparse Core Ops, SparseCore 0:
  9.5 53.1 all-gather.5
  64.2 136.9 all-gather.3
  203.4 37.8 all-gather.7
  247.2 50.5 all-reduce.1
where the time goes:
time: 308 us
  waiting for transfers between devices  238 us (77%)
  matrix products  46.8 us (15%)
  between operations  13.2 us (4%)
  blocking collectives  5 us (2%)
    all_gather x1, waiting for transfers between devices, per_device(): gathered = lax.all_gather(w_first, 'batch', axis=1, tiled=True)  139 us
    all_gather x1, waiting for transfers between devices, per_device(): lax.all_gather(w_second, 'batch', axis=1, tiled=True)  48.2 us
    psum x1, waiting for transfers between devices, per_device(): lax.psum(numer.astype(jnp.bfloat16), 'task').astype(jnp.float32)  45.5 us
    dot_general x1, matrix products, per_device(): jnp.einsum('etr,erh->eth', columns, lax.all_gather(w_second, 'batch', axi...  36.5 us
  transfers between devices with their start and end apart: 4, of which 4 were waited for; matrix products, arithmetic and copies ran while one was open for 14% of the time, Pallas kernels for 0%

commit v1 on v0

--- a/solution.py
+++ b/solution.py
@@ -40,7 +40,7 @@
     ).astype(jnp.bfloat16)
     numer = jnp.einsum("tek,eth->tkh", weights, expert_out.astype(jnp.float32))
     numer_all, total_all = (
-        lax.psum(numer.astype(jnp.bfloat16), "task").astype(jnp.float32),
+        jnp.sum(lax.all_gather(numer.astype(jnp.bfloat16), "task"), axis=0).astype(jnp.float32),
         lax.psum(gate_total.astype(jnp.bfloat16), "task").astype(jnp.float32),
     )
     first_task = lax.axis_index("task") * own_tasks

time: 308 us -> 305 us (level)
  waiting for transfers between devices: 238 us -> 231 us
  other arithmetic: 2.47 us -> 5.8 us
    psum x1 -> x0, waiting for transfers between devices: 45.5 us -> none  [per_device(): lax.psum(numer.astype(jnp.bfloat16), 'task').astype(jnp.float32)]
    all_gather x0 -> x1, waiting for transfers between devices: none -> 38.8 us  [per_device(): lax.all_gather(numer.astype(jnp.bfloat16), 'task')]
    reduce_sum x0 -> x1, other arithmetic: none -> 4.45 us  [per_device(): jnp.sum(lax.all_gather(numer.astype(jnp.bfloat16), 'task'), axis=0)]
where the time goes in v1:
time: 305 us
  waiting for transfers between devices  231 us (76%)
  matrix products  47 us (15%)
  between operations  13.2 us (4%)
  other arithmetic  5.8 us (2%)
  blocking collectives  5 us (2%)
    all_gather x1, waiting for transfers between devices, per_device(): gathered = lax.all_gather(w_first, 'batch', axis=1, tiled=True)  139 us
    all_gather x1, waiting for transfers between devices, per_device(): lax.all_gather(w_second, 'batch', axis=1, tiled=True)  48.2 us
    all_gather x1, waiting for transfers between devices, per_device(): lax.all_gather(numer.astype(jnp.bfloat16), 'task')  38.8 us
    dot_general x1, matrix products, per_device(): jnp.einsum('etr,erh->eth', columns, lax.all_gather(w_second, 'batch', axi...  36.5 us
  transfers between devices with their start and end apart: 4, of which 4 were waited for; matrix products, arithmetic and copies ran while one was open for 14% of the time, Pallas kernels for 0%

profile of v1, /device:TPU:0, one launch (start us, length us, event | category | flops | bytes accessed | tf_op | source)
XLA Modules:
  0.0 304.7 jit_solution(5226708973916134222)
XLA Ops:
  6.5 0.0 copy-start
  6.5 0.0 all-gather.8.cloned.1.call-start
  6.5 0.7 all-gather.8.cloned.1.call-update
  7.3 0.0 all-gather.6.cloned.1.call-start
  7.3 0.7 all-gather.6.cloned.1.call-update
  8.0 0.0 all-gather.10.cloned.1.call-start
  8.1 0.7 all-gather.10.cloned.1.call-update
  8.7 0.0 all-gather.12.cloned.1.call-start
  8.8 0.9 reshape.6
  9.8 4.1 %fusion.30 = (bf16[768,4]{0,1:T(4,128)(2,1)S(1)}, bf16[768,4,4]{0,2,1:T(4,128)(2,1)S(1)}) fusion(bf16[4,4,3328]{2,1,0:T(4,128)(2,1)S(1)} %dot_general.26, bf16[768,3328]{1,0:T(8,128)(2,1)} %param.7), kind=kOutput, calls=%fused_computation.30 | convolution fusion | flops 81810432 | bytes 5249024 | tf_op jit(solution)/shard_map/dot_general | solution.py:16
  13.8 0.6 copy.9
  14.4 48.2 %all-gather.8.cloned.1.call-done = bf16[4,1024,512]{2,1,0:T(8,128)(2,1)} async-done(((bf16[4,64,512]{2,1,0:T(8,128)(2,1)}), bf16[4,1024,512]{2,1,0:T(8,128)(2,1)}) %all-gather.8.cloned.1.call-update) | async-done | bytes 4194320 | tf_op jit(solution)/shard_map/all_gather | solution.py:28
  62.7 138.5 %all-gather.6.cloned.1.call-done = bf16[4,3328,1024]{2,1,0:T(8,128)(2,1)} async-done(((bf16[4,208,1024]{2,1,0:T(8,128)(2,1)}), bf16[4,3328,1024]{2,1,0:T(8,128)(2,1)}) %all-gather.6.cloned.1.call-update) | async-done | bytes 27262992 | tf_op jit(solution)/shard_map/all_gather | solution.py:13
  201.2 36.5 %fusion = bf16[4,768,512]{2,1,0:T(8,128)(2,1)} fusion(bf16[4,1024,512]{2,1,0:T(8,128)(2,1)} %all-gather.8.cloned.1.call-done, bf16[4,3328,1024]{2,1,0:T(8,128)(2,1)} %all-gather.6.cloned.1.call-done, bf16[768,3328]{1,0:T(8,128)(2,1)} %param.7), kind=kOutput, calls=%fused_computation.1 | convolution fusion | flops 24165482496 | bytes 39714816 | tf_op jit(solution)/shard_map/etr,erh->eth/dot_general | solution.py:25
  237.7 3.5 %all-gather.10.cloned.1.call-done = bf16[4,512,256]{2,1,0:T(8,128)(2,1)} async-done(((bf16[4,32,256]{2,1,0:T(8,128)(2,1)}), bf16[4,512,256]{2,1,0:T(8,128)(2,1)}) %all-gather.10.cloned.1.call-update) | async-done | bytes 1048592 | tf_op jit(solution)/shard_map/all_gather | solution.py:37
  241.3 3.2 %fusion.10 = bf16[4,768,256]{2,1,0:T(8,128)(2,1)S(1)} fusion(bf16[4,512,256]{2,1,0:T(8,128)(2,1)} %all-gather.10.cloned.1.call-done, bf16[4,768,512]{2,1,0:T(8,128)(2,1)} %fusion), kind=kOutput, calls=%fused_computation.8 | convolution fusion | flops 810024960 | bytes 5767168 | tf_op jit(solution)/shard_map/etr,erh->eth/dot_general | solution.py:34
  244.4 2.7 convolution_convert_fusion
  247.1 0.0 copy-start.1
  247.1 0.0 all-gather.12.cloned.1.call-update
  247.1 5.0 %psum.7 = bf16[768,4]{0,1:T(4,128)(2,1)S(1)} all-reduce(bf16[768,4]{0,1:T(4,128)(2,1)S(1)} %get-tuple-element.5), channel_id=1, replica_groups=mesh['task'=2,'batch'=16] {'task'}, use_global_device_ids=true, to_apply=%region_2.3 | all-reduce | flops 3072 | bytes 12288 | tf_op jit(solution)/shard_map/psum | solution.py:44
  252.2 0.2 copy.10
  252.3 38.8 %all-gather.12.cloned.1.call-done = bf16[1536,4,256]{2,1,0:T(4,128)(2,1)} async-done(((bf16[768,4,256]{2,1,0:T(4,128)(2,1)}), bf16[1536,4,256]{2,1,0:T(4,128)(2,1)}) %all-gather.12.cloned.1.call-update) | async-done | bytes 3145744 | tf_op jit(solution)/shard_map/all_gather | solution.py:43
  291.2 4.4 %reduce_sum.21 = bf16[768,4,256]{2,1,0:T(4,128)(2,1)S(1)} reduce(bf16[2,768,4,256]{3,2,1,0:T(4,128)(2,1)} %bitcast.33, bf16[]{:T(256)} %constant.10.clone.1), dimensions={0}, to_apply=%region_0.1 | reduce | flops 786432 | bytes 4718594 | tf_op jit(solution)/shard_map/reduce_sum | solution.py:43
  295.6 1.3 fusion.14
  297.0 0.0 copy-done
  297.0 0.0 copy-done.1
  297.0 0.5 fusion.18
  297.5 0.6 copy.25
  (2 shorter events, 0.0 us)
Async XLA Ops:
  6.5 290.4 %copy-start = (bf16[2,256,128]{2,1,0:T(8,128)(2,1)S(1)}, bf16[2,256,128]{2,1,0:T(8,128)(2,1)}, u32[]{:S(2)}) copy-start(bf16[2,256,128]{2,1,0:T(8,128)(2,1)} %param.12) | copy-start | bytes 393220
  6.5 56.1 %all-gather.8.cloned.1.call-start = ((), (), s32[]{:S(2)}) async-start(), calls=%async_computation.1 | async-start | bytes 4456448 | tf_op jit(solution)/shard_map/all_gather | solution.py:28
  7.3 193.9 %all-gather.6.cloned.1.call-start = ((), (), s32[]{:S(2)}) async-start(), calls=%async_computation | async-start | bytes 28966912 | tf_op jit(solution)/shard_map/all_gather | solution.py:13
  8.0 233.3 %all-gather.10.cloned.1.call-start = ((), (), s32[]{:S(2)}) async-start(), calls=%async_computation.2 | async-start | bytes 1114112 | tf_op jit(solution)/shard_map/all_gather | solution.py:37
  8.7 282.4 %all-gather.12.cloned.1.call-start = ((), (), s32[]{:S(2)}) async-start(), calls=%async_computation.3 | async-start | bytes 4718592 | tf_op jit(solution)/shard_map/all_gather | solution.py:43
  247.1 49.9 %copy-start.1 = (bf16[2,128]{1,0:T(2,128)(2,1)S(1)}, bf16[2,128]{1,0:T(2,128)(2,1)}, u32[]{:S(2)}) copy-start(bf16[2,128]{1,0:T(2,128)(2,1)} %param.13) | copy-start | bytes 1540
Sparse Core Ops, SparseCore 0:
  9.5 53.1 all-gather.7
  64.2 136.9 all-gather.5
  203.4 37.8 all-gather.9
  247.3 43.8 all-gather.11
